TPU v7x, 256 devices: a whole 4x4x8 slice. The times are simulated.
256 devices in a mesh: gx: 8 (over y_hi, x), gy: 8 (over z), gz: 4 (over y_lo, core).
Axes of the slice: x: 4, y: 4 (y_hi: 2, y_lo: 2; y = y_hi * 2 + y_lo), z: 8, core: 2. Of those that a mesh axis runs over, the one named last changes fastest.
Arguments:
- volume: float32 [16, 32, 128, 512], P(None, 'gx', 'gy', 'gz'), may hold values from -26 to 26
- weight: float32 [16, 16, 3, 3, 3], replicated, may hold values from -0.3125 to 0.3125
- gamma: float32 [16], replicated, may hold values from 0.5 to 1.5
- beta: float32 [16], replicated, may hold values from -0.5 to 0.5
- cotangent: float32 [16, 32, 128, 512], P(None, 'gx', 'gy', 'gz'), may hold values from -6 to 6
Outputs:
- input_grad: float32 [16, 32, 128, 512], P(None, 'gx', 'gy', 'gz')
- weight_grad: float32 [16, 16, 3, 3, 3], replicated
- gamma_grad: float32 [16], replicated
- beta_grad: float32 [16], replicated
All inputs are finite; a program needn't handle non-finite values.
Results may differ from a plain program's by a relative error of at most 0.0003.
Values sent between devices are 32-bit elements; how exact they have to be, the bound alone decides.
A program may use at most 64 MiB of HBM per device.

v0:
```python
import functools

import jax
import jax.numpy as jnp
from jax import lax
from jax.experimental import pallas as pl
from jax.experimental.pallas import tpu as pltpu
from jax.sharding import PartitionSpec as P

MESH = pl.DeviceIdType.MESH
L = 128
C = 16
ROWS = 9 * C
BF = jnp.bfloat16
F32 = jnp.float32
SIDES = [(sx, sy) for sx in (-1, 0, 1) for sy in (-1, 0, 1) if (sx, sy) != (0, 0)]


def split(v):
    hi = v.astype(BF)
    lo = (v - hi.astype(F32)).astype(BF)
    return hi, lo


def kernel(
    dims, count, vol_ref, cot_ref, mf_ref, mb_ref, gain_ref, shift_ref,
    out_ref, aux_ref,
    vin, cin, ev, ec, eo, ea, hv, hc, ho, ha, cbv, cbc, cbo,
    r_ref, o_ref, agp, cvp, acc_ref, gw,
    s1x, s1y, s1z, s2x, s2y, s2z, gx_buf, gy_buf, gz_buf, gf_buf,
    in_sem, hsend, hrecv, asend, arecv, gsend, grecv,
):
    nx, ny, nz, X, Y = dims
    W = (Y + 2) * L
    I0, I1 = L, (Y + 1) * L
    mx, my, mz = lax.axis_index("gx"), lax.axis_index("gy"), lax.axis_index("gz")
    lane = lax.broadcasted_iota(jnp.int32, (C, L), 1)

    def near(m, s, n):
        return lax.rem(m + (s + n), n)

    def side_id(sx, sy):
        out = {}
        if sx:
            out["gx"] = near(mx, sx, nx)
        if sy:
            out["gy"] = near(my, sy, ny)
        return out

    load_v = pltpu.make_async_copy(vol_ref, vin, in_sem.at[0])
    load_c = pltpu.make_async_copy(cot_ref, cin, in_sem.at[1])
    load_v.start()
    load_c.start()

    barrier = pltpu.get_barrier_semaphore()
    greets = 0
    for axis, m, n in (("gx", mx, nx), ("gy", my, ny), ("gz", mz, nz)):
        for d in range(1, n):
            pl.semaphore_signal(
                barrier, inc=1, device_id={axis: lax.rem(m + d, n)}, device_id_type=MESH
            )
            greets += 1
    for sx, sy in SIDES:
        if sx and sy:
            pl.semaphore_signal(barrier, inc=1, device_id=side_id(sx, sy), device_id_type=MESH)
            greets += 1

    def face(ref, sx, sy):
        src_x = {1: X, -1: 1, 0: pl.ds(1, X)}[sx]
        dst_x = {1: 0, -1: X + 1, 0: pl.ds(1, X)}[sx]
        src_y = {1: pl.ds(Y * L, L), -1: pl.ds(L, L), 0: pl.ds(I0, Y * L)}[sy]
        dst_y = {1: pl.ds(0, L), -1: pl.ds(I1, L), 0: pl.ds(I0, Y * L)}[sy]
        return ref.at[src_x, :, src_y], ref.at[dst_x, :, dst_y]

    def face_copy(which, ref, k):
        sx, sy = SIDES[k]
        src, dst = face(ref, sx, sy)
        return pltpu.make_async_remote_copy(
            src_ref=src, dst_ref=dst, send_sem=hsend.at[which, k], recv_sem=hrecv.at[which, k],
            device_id=side_id(sx, sy), device_id_type=MESH,
        )

    def col_copy(which, cb, h, k):
        s = 1 - 2 * k
        return pltpu.make_async_remote_copy(
            src_ref=cb.at[k], dst_ref=h.at[4, k],
            send_sem=hsend.at[which, 8 + k], recv_sem=hrecv.at[which, 8 + k],
            device_id={"gz": near(mz, s, nz)}, device_id_type=MESH,
        )

    def tile_copy(which, h, k):
        sx, sy = SIDES[k]
        return pltpu.make_async_remote_copy(
            src_ref=h.at[4], dst_ref=h.at[(1 - sx) * 3 + (1 - sy)],
            send_sem=hsend.at[which, 10 + k], recv_sem=hrecv.at[which, 10 + k],
            device_id=side_id(sx, sy), device_id_type=MESH,
        )

    def send_cols(which, cb, h):
        for k in range(2):
            col_copy(which, cb, h, k).start()

    def send_faces(which, e):
        for k in (1, 6, 3, 4, 0, 2, 5, 7):
            face_copy(which, e, k).start()

    def pass_tiles(which, cb, h):
        for k in range(2):
            col_copy(which, cb, h, k).wait_recv()
        for k in range(8):
            tile_copy(which, h, k).start()

    def wait_halo(which, e, h):
        for k in range(8):
            face_copy(which, e, k).wait_recv()
        for k in range(8):
            tile_copy(which, h, k).wait_recv()

    def drain_halo(which, e, cb, h):
        for k in range(8):
            face_copy(which, e, k).wait_send()
        for k in range(2):
            col_copy(which, cb, h, k).wait_send()
        for k in range(8):
            tile_copy(which, h, k).wait_send()

    def peer(buf, axis, m, n, ss, rs, d, arriving=False):
        slot = lax.rem(m + (n - d), n) if arriving else m
        return pltpu.make_async_remote_copy(
            src_ref=buf.at[m], dst_ref=buf.at[slot], send_sem=ss.at[d], recv_sem=rs.at[d],
            device_id={axis: lax.rem(m + d, n)}, device_id_type=MESH,
        )

    def arrive(buf, axis, m, n, ss, rs):
        for d in range(1, n):
            peer(buf, axis, m, n, ss, rs, d, True).wait_recv()

    def start(spec, value):
        buf, _, m, n = spec[:4]
        buf[m] = value
        for d in range(1, n):
            peer(*spec, d).start()

    def finish(spec):
        arrive(*spec)
        total = spec[0][0]
        for j in range(1, spec[3]):
            total = total + spec[0][j]
        return total

    def settle(spec):
        for d in range(1, spec[3]):
            peer(*spec, d).wait_send()

    stage = {
        (0, 0): (s1x, "gx", mx, nx, asend.at[0], arecv.at[0]),
        (0, 1): (s1y, "gy", my, ny, asend.at[1], arecv.at[1]),
        (0, 2): (s1z, "gz", mz, nz, asend.at[2], arecv.at[2]),
        (1, 0): (s2x, "gx", mx, nx, asend.at[3], arecv.at[3]),
        (1, 1): (s2y, "gy", my, ny, asend.at[4], arecv.at[4]),
        (1, 2): (s2z, "gz", mz, nz, asend.at[5], arecv.at[5]),
    }
    g_y = (gy_buf, "gy", my, ny, gsend.at[1], grecv.at[1])
    g_z = (gz_buf, "gz", mz, nz, gsend.at[2], grecv.at[2])
    g_f = (gf_buf, "gx", mx, nx, gsend.at[3], grecv.at[3])

    def pack(columns):
        tile = jnp.zeros((8, L), F32)
        lane8 = lane[0:8]
        for j, col in enumerate(columns):
            for half in range(2):
                tile = jnp.where(lane8 == 2 * j + half, col[8 * half : 8 * half + 8], tile)
        return tile

    def unpack(tile, j):
        lane8 = lane[0:8]
        return jnp.concatenate(
            [
                jnp.sum(jnp.where(lane8 == 2 * j + half, tile, 0.0), axis=1, keepdims=True)
                for half in range(2)
            ],
            axis=0,
        )

    def bring(src, e, cb):
        def body(x, cols):
            right, left = cols
            for y in range(Y):
                t = src[pl.ds(x * Y + y, C, stride=X * Y), :]
                e[x + 1, :, (y + 1) * L : (y + 2) * L] = t
                at = x * Y + y
                here = lane == at
                right = jnp.where(here, pltpu.roll(t, lax.rem(at + 1, L), 1), right)
                left = jnp.where(here, pltpu.roll(t, at, 1), left)
            return right, left

        zero = jnp.zeros((C, L), F32)
        right, left = lax.fori_loop(0, X, body, (zero, zero))
        cb[0] = right
        cb[1] = left

    def columns_of(e, cb):
        def body(x, cols):
            right, left = cols
            for y in range(Y):
                t = e[x + 1, :, (y + 1) * L : (y + 2) * L]
                at = x * Y + y
                here = lane == at
                right = jnp.where(here, pltpu.roll(t, lax.rem(at + 1, L), 1), right)
                left = jnp.where(here, pltpu.roll(t, at, 1), left)
            return right, left

        zero = jnp.zeros((C, L), F32)
        right, left = lax.fori_loop(0, X, body, (zero, zero))
        cb[0] = right
        cb[1] = left

    def build(e, h, xp, dx, xs, blocks):
        for yb in blocks:
            dy = -1 if yb == 0 else (1 if yb == Y + 1 else 0)
            ys = Y - 1 if yb == 0 else (0 if yb == Y + 1 else yb - 1)
            slot = (dx + 1) * 3 + dy + 1
            at = xs * Y + ys
            t = e[xp, :, yb * L : (yb + 1) * L]
            before = pltpu.roll(h[slot, 0], lax.rem(L - at, L), 1)
            after = pltpu.roll(h[slot, 1], lax.rem(2 * L - 1 - at, L), 1)
            low = jnp.where(lane == 0, before, pltpu.roll(t, 1, 1))
            high = jnp.where(lane == L - 1, after, pltpu.roll(t, L - 1, 1))
            for c, v in enumerate((low, t, high)):
                hi, lo = split(v)
                r_ref[xp, c * C : (c + 1) * C, yb * L : (yb + 1) * L] = hi
                r_ref[xp, (3 + c) * C : (4 + c) * C, yb * L : (yb + 1) * L] = lo

    def taps(xp, lo, hi):
        r = r_ref[xp, :, lo:hi]
        return jnp.concatenate([r, r[0 : 3 * C]], axis=0)

    def spread(m_ref, xp, lo, hi, which):
        part = jnp.dot(
            m_ref[which[0] * 3 * C : (which[-1] + 1) * 3 * C, :], taps(xp, lo, hi),
            preferred_element_type=F32,
        )
        for ia, a in enumerate(which):
            for b in range(3):
                row = (ia * 3 + b) * C
                at = lo + (2 - b) * L
                o_ref[xp - a + 2, :, at : at + hi - lo] += part[row : row + C]

    def clear():
        def body(x, carry):
            o_ref[x] = jnp.zeros((C, (Y + 4) * L), F32)
            return carry

        lax.fori_loop(0, X + 4, body, 0)

    def interior(m_ref, e, h):
        def body(x, carry):
            build(e, h, x + 1, 0, x, range(1, Y + 1))
            spread(m_ref, x + 1, I0, I1, (0, 1, 2))
            return carry

        lax.fori_loop(0, X, body, 0)

    def rim(m_ref, e, h):
        build(e, h, 0, -1, X - 1, range(Y + 2))
        spread(m_ref, 0, 0, W, (0,))
        build(e, h, X + 1, 1, 0, range(Y + 2))
        spread(m_ref, X + 1, 0, W, (2,))

        def body(x, carry):
            build(e, h, x + 1, 0, x, (0, Y + 1))
            spread(m_ref, x + 1, 0, L, (0, 1, 2))
            spread(m_ref, x + 1, I1, I1 + L, (0, 1, 2))
            return carry

        lax.fori_loop(0, X, body, 0)

    def clear_pad(ref):
        for x in range(X + 4):
            if x < 2 or x >= X + 2:
                ref[x] = jnp.zeros((2 * C, (Y + 4) * L), BF)
            else:
                ref[x, :, 0 : 2 * L] = jnp.zeros((2 * C, 2 * L), BF)
                ref[x, :, (Y + 2) * L : (Y + 4) * L] = jnp.zeros((2 * C, 2 * L), BF)

    def put_pad(ref, x, v):
        hi, lo = split(v)
        ref[x + 2, 0:C, 2 * L : (Y + 2) * L] = hi
        ref[x + 2, C : 2 * C, 2 * L : (Y + 2) * L] = lo

    def correlate(ref):
        acc_ref[...] = jnp.zeros((2 * ROWS, L), F32)

        def body(xp, carry):
            left = jnp.concatenate(
                [
                    ref[xp - a + 2, :, (2 - b) * L : (2 - b) * L + W]
                    for a in range(3)
                    for b in range(3)
                ],
                axis=0,
            )
            acc_ref[:, 0 : 6 * C] += lax.dot_general(
                left, r_ref[xp], (((1,), (1,)), ((), ())), preferred_element_type=F32
            )
            return carry

        lax.fori_loop(0, X + 2, body, 0)
        pieces = []
        for k in range(9):
            t = acc_ref[2 * k * C : (2 * k + 1) * C] + acc_ref[(2 * k + 1) * C : (2 * k + 2) * C]
            pieces.append(t + pltpu.roll(t, L - 3 * C, 1))
        return pieces

    clear()
    clear_pad(agp)
    clear_pad(cvp)
    load_v.wait()
    bring(vin, ev, cbv)
    pl.semaphore_wait(barrier, greets)
    send_cols(0, cbv, hv)
    send_faces(0, ev)
    load_c.wait()
    bring(cin, ec, cbc)
    pass_tiles(0, cbv, hv)
    send_cols(1, cbc, hc)
    send_faces(1, ec)
    interior(mf_ref, ev, hv)

    def vol_sum(x, s):
        return s + jnp.sum(ev[x + 1, :, I0:I1], axis=1, keepdims=True)

    in_sum = lax.fori_loop(0, X, vol_sum, jnp.zeros((C, 1), F32))
    wait_halo(0, ev, hv)
    rim(mf_ref, ev, hv)

    def gather_conv(x, sums):
        s, q = sums
        t = o_ref[x + 2, :, 2 * L : (Y + 2) * L]
        eo[x + 1, :, I0:I1] = t
        return (
            s + jnp.sum(t, axis=1, keepdims=True),
            q + jnp.sum(t * t, axis=1, keepdims=True),
        )

    zero_col = jnp.zeros((C, 1), F32)
    s, q = lax.fori_loop(0, X, gather_conv, (zero_col, zero_col))
    start(stage[0, 0], pack((s, q, in_sum)))
    columns_of(eo, cbo)
    send_cols(2, cbo, ho)
    send_faces(2, eo)

    def pad_conv(x, carry):
        put_pad(cvp, x, eo[x + 1, :, I0:I1])
        return carry

    lax.fori_loop(0, X, pad_conv, 0)
    part = finish(stage[0, 0])
    start(stage[0, 1], part)
    cross = correlate(cvp)
    for k in range(9):
        gw[k * C : (k + 1) * C] = pltpu.roll(cross[k], L // 2, 1)
    clear()
    pass_tiles(1, cbc, hc)
    part = finish(stage[0, 1])
    start(stage[0, 2], part)
    pass_tiles(2, cbo, ho)
    total1 = finish(stage[0, 2])
    mean = unpack(total1, 0) / count
    var = unpack(total1, 1) / count - mean * mean
    rstd = lax.rsqrt(var + 1e-05)
    gain = gain_ref[...]
    shift = shift_ref[...]

    def slope(conv, cot):
        normed = (conv - mean) * rstd
        act = gain * normed + shift
        sig = 1.0 / (1.0 + jnp.exp(-act))
        return cot * sig * (1.0 + act * (1.0 - sig)), normed

    def local_slope(x, sums):
        sg, sb = sums
        a, normed = slope(eo[x + 1, :, I0:I1], ec[x + 1, :, I0:I1])
        ea[x + 1, :, I0:I1] = a
        put_pad(agp, x, a)
        return (
            sg + jnp.sum(a * normed, axis=1, keepdims=True),
            sb + jnp.sum(a, axis=1, keepdims=True),
        )

    sg, sb = lax.fori_loop(0, X, local_slope, (zero_col, zero_col))
    start(stage[1, 0], pack((sg, sb)))
    cross = correlate(agp)
    for k in range(9):
        g = jnp.where(lane < L // 2, cross[k], gw[k * C : (k + 1) * C])
        gw[k * C : (k + 1) * C] = g
    tail = gw.shape[0] - ROWS
    if tail:
        gw[ROWS:] = jnp.zeros((tail, L), F32)
    chunk = gw.shape[0] // nx

    def piece(j):
        return gw.at[pl.ds(pl.multiple_of(j * chunk, 8), chunk)]

    gx_buf[mx] = gw[pl.ds(pl.multiple_of(mx * chunk, 8), chunk)]

    def scatter(d, arriving=False):
        to = lax.rem(mx + d, nx)
        slot = lax.rem(mx + (nx - d), nx) if arriving else mx
        return pltpu.make_async_remote_copy(
            src_ref=piece(to), dst_ref=gx_buf.at[slot],
            send_sem=gsend.at[0, d], recv_sem=grecv.at[0, d],
            device_id={"gx": to}, device_id_type=MESH,
        )

    part = finish(stage[1, 0])
    start(stage[1, 1], part)
    for d in range(1, nx):
        scatter(d).start()

    wait_halo(1, ec, hc)
    wait_halo(2, eo, ho)
    for xp in (0, X + 1):
        a, _ = slope(eo[xp], ec[xp])
        ea[xp] = a

    def edge_slope(x, carry):
        for at in (0, I1):
            a, _ = slope(eo[x + 1, :, at : at + L], ec[x + 1, :, at : at + L])
            ea[x + 1, :, at : at + L] = a
        return carry

    lax.fori_loop(0, X, edge_slope, 0)

    def tile_slope(k, carry):
        for j in range(2):
            a, _ = slope(ho[k, j], hc[k, j])
            ha[k, j] = a
        return carry

    lax.fori_loop(0, 9, tile_slope, 0)

    part = finish(stage[1, 1])
    start(stage[1, 2], part)
    for d in range(1, nx):
        scatter(d, True).wait_recv()
    gpart = gx_buf[0]
    for j in range(1, nx):
        gpart = gpart + gx_buf[j]
    start(g_y, gpart)
    total2 = finish(stage[1, 2])
    gain_grad = unpack(total2, 0)
    shift_grad = unpack(total2, 1)
    scale = gain * rstd
    k_conv = -scale * rstd * (gain_grad / count)
    k_one = -scale * (shift_grad / count) - k_conv * mean

    def blend(xp, carry):
        ea[xp] = scale * ea[xp] + k_conv * eo[xp] + k_one
        return carry

    lax.fori_loop(0, X + 2, blend, 0)

    def blend_tile(k, carry):
        for j in range(2):
            ha[k, j] = scale * ha[k, j] + k_conv * ho[k, j] + k_one
        return carry

    lax.fori_loop(0, 9, blend_tile, 0)
    gpart = finish(g_y)
    start(g_z, gpart)
    interior(mb_ref, ea, ha)
    gpart = finish(g_z)
    start(g_f, gpart)
    rim(mb_ref, ea, ha)

    def emit(x, carry):
        out_ref[x] = o_ref[x + 2, :, 2 * L : (Y + 2) * L]
        return carry

    lax.fori_loop(0, X, emit, 0)
    aux_ref[0:8] = total1
    aux_ref[8:16] = total2
    arrive(*g_f)
    for j in range(nx):
        aux_ref[16 + j * chunk : 16 + (j + 1) * chunk] = gf_buf[j]

    drain_halo(0, ev, cbv, hv)
    drain_halo(1, ec, cbc, hc)
    drain_halo(2, eo, cbo, ho)
    for key in stage:
        settle(stage[key])
    for d in range(1, nx):
        scatter(d).wait_send()
    for spec in (g_y, g_z, g_f):
        settle(spec)


def shards(sizes, volume, weight, gamma, beta, cotangent):
    nx, ny, nz = sizes
    _, X, Y, Z = volume.shape
    count = float(X * Y * Z * nx * ny * nz)
    W = (Y + 2) * L
    chunk = -(-(ROWS // 8) // nx) * 8
    rows = chunk * nx

    def stack(w):
        hi = w.astype(BF).astype(F32)
        lo = w - hi
        return jnp.concatenate([hi, hi, lo], axis=1).astype(BF)

    forward = stack(weight.transpose(2, 3, 0, 4, 1).reshape(ROWS, 3 * C))
    backward = stack(
        weight[:, :, ::-1, ::-1, ::-1].transpose(2, 3, 1, 4, 0).reshape(ROWS, 3 * C)
    )
    vmem = pl.BlockSpec(memory_space=pltpu.VMEM)
    hbm = pl.BlockSpec(memory_space=pl.ANY)
    e_shape = pltpu.VMEM((X + 2, C, W), F32)
    h_shape = pltpu.VMEM((9, 2, C, L), F32)
    cb_shape = pltpu.VMEM((2, C, L), F32)
    pad_shape = pltpu.VMEM((X + 4, 2 * C, (Y + 4) * L), BF)
    dma = pltpu.SemaphoreType.DMA
    most = max(nx, ny, nz)
    blocks, aux = pl.pallas_call(
        functools.partial(kernel, (nx, ny, nz, X, Y), count),
        out_shape=(
            jax.ShapeDtypeStruct((X, C, Y * L), F32),
            jax.ShapeDtypeStruct((16 + rows, L), F32),
        ),
        in_specs=[hbm, hbm, vmem, vmem, vmem, vmem],
        out_specs=(vmem, vmem),
        scratch_shapes=[
            pltpu.VMEM((C * X * Y, L), F32), pltpu.VMEM((C * X * Y, L), F32),
            e_shape, e_shape, e_shape, e_shape,
            h_shape, h_shape, h_shape, h_shape,
            cb_shape, cb_shape, cb_shape,
            pltpu.VMEM((X + 2, 6 * C, W), BF),
            pltpu.VMEM((X + 4, C, (Y + 4) * L), F32),
            pad_shape, pad_shape,
            pltpu.VMEM((2 * ROWS, L), F32),
            pltpu.VMEM((rows, L), F32),
            pltpu.VMEM((nx, 8, L), F32), pltpu.VMEM((ny, 8, L), F32), pltpu.VMEM((nz, 8, L), F32),
            pltpu.VMEM((nx, 8, L), F32), pltpu.VMEM((ny, 8, L), F32), pltpu.VMEM((nz, 8, L), F32),
            pltpu.VMEM((nx, chunk, L), F32), pltpu.VMEM((ny, chunk, L), F32),
            pltpu.VMEM((nz, chunk, L), F32), pltpu.VMEM((nx, chunk, L), F32),
            dma((2,)), dma((3, 18)), dma((3, 18)), dma((6, most)), dma((6, most)),
            dma((4, most)), dma((4, most)),
        ],
        compiler_params=pltpu.CompilerParams(
            collective_id=0, has_side_effects=True, vmem_limit_bytes=60 << 20
        ),
    )(
        volume.reshape(C * X * Y, L), cotangent.reshape(C * X * Y, L), forward, backward,
        gamma.reshape(C, 1), beta.reshape(C, 1),
    )
    input_grad = blocks.reshape(X, C, Y, L).transpose(1, 0, 2, 3)

    def column(base, j):
        return jnp.concatenate([aux[base : base + 8, 2 * j], aux[base : base + 8, 2 * j + 1]])

    mean = column(0, 0) / count
    var = column(0, 1) / count - mean * mean
    input_total = column(0, 2)
    rstd = lax.rsqrt(var + 1e-05)
    gamma_grad = column(8, 0)
    beta_grad = column(8, 1)
    scale = gamma * rstd
    both = aux[16 : 16 + ROWS]

    def taps(lo):
        return both[:, lo : lo + 3 * C].reshape(3, 3, C, 3, C).transpose(2, 4, 0, 1, 3)

    def out(v):
        return v[:, None, None, None, None]

    wide = input_total[None, :, None, None, None]
    norm_total = out(rstd) * (taps(L // 2) - out(mean) * wide)
    weight_grad = out(scale) * (
        taps(0) - out(beta_grad / count) * wide - out(gamma_grad / count) * norm_total
    )
    return (input_grad, weight_grad, gamma_grad, beta_grad)


def solution(mesh):
    sizes = tuple(mesh.shape[name] for name in ("gx", "gy", "gz"))
    spec = P(None, "gx", "gy", "gz")
    return jax.shard_map(
        functools.partial(shards, sizes),
        mesh=mesh,
        in_specs=(spec, P(), P(), P(), spec),
        out_specs=(spec, P(), P(), P()),
        check_vma=False,
    )
```

profile of v0, /device:TPU:1, one launch (start us, length us, event | category | flops | bytes accessed | tf_op | source)
XLA Modules:
  0.0 76.4 jit_solution(5403554300034671878)
XLA Ops:
  0.6 0.0 copy-start.3
  0.6 0.6 copy-done.3
  1.3 0.0 copy-start.2
  1.3 0.7 copy.39.shift_ref
  1.9 0.0 copy-done.2
  1.9 0.7 copy.38.gain_ref
  2.6 0.9 %reverse_bitcast_fusion = f32[3,3,16,3,16]{2,4,3,1,0:T(8,128)S(1)} fusion(f32[16,16,3,3,3]{1,0,4,3,2:T(8,128)} %param.6), kind=kLoop, calls=%fused_computation.2 | loop fusion | bytes 55296 | tf_op jit(solution)/shard_map/transpose | solution.py:514
  3.6 0.1 copy.33
  3.7 0.2 reshape.181
  3.9 0.0 copy-start
  3.9 0.1 copy.36
  4.0 0.1 copy.35
  4.1 0.7 copy-done
  4.8 0.2 copy.28
  5.0 0.2 reshape.180
  5.1 0.1 copy.31
  5.2 0.1 copy.30
  5.4 0.8 %pad_maximum_fusion = (bf16[144,144]{1,0:T(8,128)(2,1)}, bf16[144,144]{1,0:T(8,128)(2,1)}) fusion(bf16[144,48]{1,0:T(8,128)(2,1)S(1)} %subtract_convert_fusion.1, bf16[144,48]{1,0:T(8,128)(2,1)S(1)} %copy.31, bf16[144,48]{1,0:T(8,128)(2,1)S(1)} %subtract_convert_fusion, bf16[144,48]{1,0:T(8,128)(2,1)S(1)} %copy.36), kind=kLoop, calls=%fused_computation.3 | loop fusion | flops 248832 | bytes 138240 | tf_op jit(solution)/shard_map/concatenate | solution.py:510
  6.2 64.9 %shard_map.84 = (f32[4,16,2048]{2,1,0:T(8,128)}, f32[208,128]{1,0:T(8,128)}) custom-call(f32[1024,128]{1,0:T(8,128)} %bitcast.29, f32[1024,128]{1,0:T(8,128)} %bitcast.30, bf16[144,144]{1,0:T(8,128)(2,1)} %get-tuple-element.37.mf_ref, bf16[144,144]{1,0:T(8,128)(2,1)} %get-tuple-element.38.mb_ref, f32[16,1]{1,0:T(8,128)} %copy.38.gain_ref, ...), custom_call_target="tpu_custom_call" | custom-call | tf_op jit(solution)/shard_map/pallas_call | solution.py:524
  71.1 1.1 %copy.44 = f32[8,8,16,128]{3,2,1,0:T(8,128)S(1)} copy(f32[8,8,16,128]{3,1,2,0:T(8,128)} %bitcast.31) | data formatting | bytes 1048576
  72.2 0.0 copy-start.1
  72.2 0.8 %copy_bitcast_fusion = f32[16,4,16,128]{3,2,1,0:T(8,128)} fusion(f32[4,16,16,128]{3,2,1,0:T(8,128)S(1)} %bitcast.27), kind=kLoop, calls=%fused_computation | loop fusion | bytes 1048576 | tf_op jit(solution)/shard_map/transpose | solution.py:556
  73.1 0.0 copy-done.1
  73.1 0.3 slice_reduce_fusion.5
  73.4 0.6 broadcast_multiply_fusion.3
  74.0 0.1 pad_maximum_fusion.3
  74.1 0.6 broadcast_multiply_fusion.2
  74.7 0.1 fusion.1
  74.8 0.1 broadcast_multiply_fusion.1
  74.9 0.1 fusion.2
  74.9 0.1 copy.41
  75.0 0.1 copy.42
  75.1 0.2 reshape.186
  75.3 0.2 reshape.185
  75.5 0.1 multiply_bitcast_fusion
  75.6 0.8 %copy.43 = f32[16,16,3,3,3]{1,0,4,3,2:T(8,128)} copy(f32[16,16,3,3,3]{0,3,2,1,4:T(4,128)S(1)} %multiply_bitcast_fusion) | data formatting | bytes 55296
  (4 shorter events, 0.0 us)
Async XLA Ops:
  0.6 0.7 copy-start.3
  1.3 0.7 copy-start.2
  3.9 0.9 %copy-start = (f32[16,16,3,3,3]{1,0,4,3,2:T(8,128)S(1)}, f32[16,16,3,3,3]{1,0,4,3,2:T(8,128)}, u32[]{:S(2)}) copy-start(f32[16,16,3,3,3]{1,0,4,3,2:T(8,128)} %param.6) | copy-start | bytes 82948
  72.2 0.9 %copy-start.1 = (f32[208,128]{1,0:T(8,128)S(1)}, f32[208,128]{1,0:T(8,128)}, u32[]{:S(2)}) copy-start(f32[208,128]{1,0:T(8,128)} %get-tuple-element.7) | copy-start | bytes 319492
where the time goes:
time: 76.7 us; the launch traced here: 76.4 us
  Pallas kernels  64.9 us (85%)
  local copies, waits for them, and re-layouts  8.39 us (11%)
  other arithmetic  2.38 us (3%)
    pallas_call x1, Pallas kernels, shards(): pl.pallas_call(functools.partial(kernel, (nx, ny, nz, X, Y), count), out_...  64.9 us
    unnamed x10, local copies, waits for them, and re-layouts  3.34 us

commit v1 on v0

v1 whole, which is shorter than its diff:
```python
import functools

import jax
import jax.numpy as jnp
from jax import lax
from jax.experimental import pallas as pl
from jax.experimental.pallas import tpu as pltpu
from jax.sharding import PartitionSpec as P

MESH = pl.DeviceIdType.MESH
L = 128
C = 16
ROWS = 9 * C
BF = jnp.bfloat16
F32 = jnp.float32
SIDES = [(sx, sy) for sx in (-1, 0, 1) for sy in (-1, 0, 1) if (sx, sy) != (0, 0)]


def split(v):
    hi = v.astype(BF)
    lo = (v - hi.astype(F32)).astype(BF)
    return hi, lo


def kernel(
    dims, count, vol_ref, cot_ref, w_ref, gain_ref, shift_ref,
    out_ref, wout_ref, gout_ref, bout_ref,
    vin, cin, wv, gv, bv, mf_ref, mb_ref, ev, ec, eo, ea, hv, hc, ho, ha, cbv, cbc, cbo,
    r_ref, o_ref, agp, cvp, acc_ref, gw, gfull,
    z1, p1, z2, p2, gp_buf, gy_buf, gf_buf,
    in_sem, hsend, hrecv, asend, arecv, gsend, grecv,
):
    nx, ny, nz, X, Y = dims
    W = (Y + 2) * L
    I0, I1 = L, (Y + 1) * L
    mx, my, mz = lax.axis_index("gx"), lax.axis_index("gy"), lax.axis_index("gz")
    lane = lax.broadcasted_iota(jnp.int32, (C, L), 1)
    sub = lax.broadcasted_iota(jnp.int32, (C, L), 0)
    half = L // 2
    npl = nx * nz
    mp = mx * nz + mz

    def plane_id(q):
        return {"gx": lax.div(q, nz), "gz": lax.rem(q, nz)}

    def line_id(q):
        return {"gy": q}

    plane = (plane_id, mp, npl)
    line = (line_id, my, ny)

    def near(m, s, n):
        return lax.rem(m + (s + n), n)

    def side_id(sx, sy):
        out = {}
        if sx:
            out["gx"] = near(mx, sx, nx)
        if sy:
            out["gy"] = near(my, sy, ny)
        return out

    loads = [
        pltpu.make_async_copy(src, dst, in_sem.at[k])
        for k, (src, dst) in enumerate(
            ((vol_ref, vin), (cot_ref, cin), (w_ref, wv), (gain_ref, gv), (shift_ref, bv))
        )
    ]
    for copy in loads:
        copy.start()

    barrier = pltpu.get_barrier_semaphore()
    greets = 0
    for name, m, n in (plane, line):
        for d in range(1, n):
            pl.semaphore_signal(
                barrier, inc=1, device_id=name(lax.rem(m + d, n)), device_id_type=MESH
            )
            greets += 1
    for sx, sy in SIDES:
        if sx and sy:
            pl.semaphore_signal(barrier, inc=1, device_id=side_id(sx, sy), device_id_type=MESH)
            greets += 1

    def face(ref, sx, sy):
        src_x = {1: X, -1: 1, 0: pl.ds(1, X)}[sx]
        dst_x = {1: 0, -1: X + 1, 0: pl.ds(1, X)}[sx]
        src_y = {1: pl.ds(Y * L, L), -1: pl.ds(L, L), 0: pl.ds(I0, Y * L)}[sy]
        dst_y = {1: pl.ds(0, L), -1: pl.ds(I1, L), 0: pl.ds(I0, Y * L)}[sy]
        return ref.at[src_x, :, src_y], ref.at[dst_x, :, dst_y]

    def face_copy(which, ref, k):
        sx, sy = SIDES[k]
        src, dst = face(ref, sx, sy)
        return pltpu.make_async_remote_copy(
            src_ref=src, dst_ref=dst, send_sem=hsend.at[which, k], recv_sem=hrecv.at[which, k],
            device_id=side_id(sx, sy), device_id_type=MESH,
        )

    def col_copy(which, cb, k):
        s = 1 - 2 * k
        return pltpu.make_async_remote_copy(
            src_ref=cb.at[k], dst_ref=cb.at[2 + k],
            send_sem=hsend.at[which, 8 + k], recv_sem=hrecv.at[which, 8 + k],
            device_id={"gz": near(mz, s, nz)}, device_id_type=MESH,
        )

    def tile_copy(which, h, k):
        sx, sy = SIDES[k]
        return pltpu.make_async_remote_copy(
            src_ref=h.at[4], dst_ref=h.at[(1 - sx) * 3 + (1 - sy)],
            send_sem=hsend.at[which, 10 + k], recv_sem=hrecv.at[which, 10 + k],
            device_id=side_id(sx, sy), device_id_type=MESH,
        )

    def send_cols(which, cb):
        for k in range(2):
            col_copy(which, cb, k).start()

    def send_faces(which, e):
        for k in (1, 6, 3, 4, 0, 2, 5, 7):
            face_copy(which, e, k).start()

    def pass_tiles(which, cb, h):
        for k in range(2):
            col_copy(which, cb, k).wait_recv()
        h[4] = jnp.where(lane < half, cb[2], cb[3])
        for k in range(8):
            tile_copy(which, h, k).start()

    def wait_halo(which, e, h):
        for k in range(8):
            face_copy(which, e, k).wait_recv()
        for k in range(8):
            tile_copy(which, h, k).wait_recv()

    def drain_halo(which, e, cb, h):
        for k in range(8):
            face_copy(which, e, k).wait_send()
        for k in range(2):
            col_copy(which, cb, k).wait_send()
        for k in range(8):
            tile_copy(which, h, k).wait_send()

    def peer(buf, group, ss, rs, d, arriving=False):
        name, m, n = group
        slot = lax.rem(m + (n - d), n) if arriving else m
        return pltpu.make_async_remote_copy(
            src_ref=buf.at[m], dst_ref=buf.at[slot], send_sem=ss.at[d], recv_sem=rs.at[d],
            device_id=name(lax.rem(m + d, n)), device_id_type=MESH,
        )

    def arrive(buf, group, ss, rs):
        for d in range(1, group[2]):
            peer(buf, group, ss, rs, d, True).wait_recv()

    def start(spec, value):
        spec[0][spec[1][1]] = value
        for d in range(1, spec[1][2]):
            peer(*spec, d).start()

    def finish(spec):
        arrive(*spec)
        total = spec[0][0]
        for j in range(1, spec[1][2]):
            total = total + spec[0][j]
        return total

    def settle(spec):
        for d in range(1, spec[1][2]):
            peer(*spec, d).wait_send()

    s_z1 = (z1, line, asend.at[0], arecv.at[0])
    s_p1 = (p1, plane, asend.at[1], arecv.at[1])
    s_z2 = (z2, line, asend.at[2], arecv.at[2])
    s_p2 = (p2, plane, asend.at[3], arecv.at[3])
    g_y = (gy_buf, line, gsend.at[1], grecv.at[1])
    g_f = (gf_buf, plane, gsend.at[2], grecv.at[2])

    def pack(columns):
        tile = jnp.zeros((C, L), F32)
        for j, col in enumerate(columns):
            tile = jnp.where(lane == sub + j * C, col, tile)
        return jnp.sum(tile, axis=0, keepdims=True)

    def unpack(row, j):
        return jnp.sum(jnp.where(lane == sub + j * C, row, 0.0), axis=1, keepdims=True)

    def bring(src, e, cb):
        def body(x, cols):
            right, left = cols
            for y in range(Y):
                t = src[pl.ds(x * Y + y, C, stride=X * Y), :]
                e[x + 1, :, (y + 1) * L : (y + 2) * L] = t
                at = x * Y + y
                right = jnp.where(lane == at, pltpu.roll(t, at + 1, 1), right)
                left = jnp.where(lane == at + half, pltpu.roll(t, at + half, 1), left)
            return right, left

        zero = jnp.zeros((C, L), F32)
        right, left = lax.fori_loop(0, X, body, (zero, zero))
        cb[0] = right
        cb[1] = left

    def columns_of(e, cb):
        def body(x, cols):
            right, left = cols
            for y in range(Y):
                t = e[x + 1, :, (y + 1) * L : (y + 2) * L]
                at = x * Y + y
                right = jnp.where(lane == at, pltpu.roll(t, at + 1, 1), right)
                left = jnp.where(lane == at + half, pltpu.roll(t, at + half, 1), left)
            return right, left

        zero = jnp.zeros((C, L), F32)
        right, left = lax.fori_loop(0, X, body, (zero, zero))
        cb[0] = right
        cb[1] = left

    def build(e, h, xp, dx, xs, blocks):
        for yb in blocks:
            dy = -1 if yb == 0 else (1 if yb == Y + 1 else 0)
            ys = Y - 1 if yb == 0 else (0 if yb == Y + 1 else yb - 1)
            slot = (dx + 1) * 3 + dy + 1
            at = xs * Y + ys
            t = e[xp, :, yb * L : (yb + 1) * L]
            before = pltpu.roll(h[slot], lax.rem(L - at, L), 1)
            after = pltpu.roll(h[slot], half - 1 - at, 1)
            low = jnp.where(lane == 0, before, pltpu.roll(t, 1, 1))
            high = jnp.where(lane == L - 1, after, pltpu.roll(t, L - 1, 1))
            for c, v in enumerate((low, t, high)):
                hi, lo = split(v)
                r_ref[xp, c * C : (c + 1) * C, yb * L : (yb + 1) * L] = hi
                r_ref[xp, (3 + c) * C : (4 + c) * C, yb * L : (yb + 1) * L] = lo

    def taps(xp, lo, hi):
        r = r_ref[xp, :, lo:hi]
        return jnp.concatenate([r, r[0 : 3 * C]], axis=0)

    def spread(m_ref, xp, lo, hi, which):
        part = jnp.dot(
            m_ref[which[0] * 3 * C : (which[-1] + 1) * 3 * C, :], taps(xp, lo, hi),
            preferred_element_type=F32,
        )
        for ia, a in enumerate(which):
            for b in range(3):
                row = (ia * 3 + b) * C
                at = lo + (2 - b) * L
                o_ref[xp - a + 2, :, at : at + hi - lo] += part[row : row + C]

    def clear():
        def body(x, carry):
            o_ref[x] = jnp.zeros((C, (Y + 4) * L), F32)
            return carry

        lax.fori_loop(0, X + 4, body, 0)

    def interior(m_ref, e, h):
        def body(x, carry):
            build(e, h, x + 1, 0, x, range(1, Y + 1))
            spread(m_ref, x + 1, I0, I1, (0, 1, 2))
            return carry

        lax.fori_loop(0, X, body, 0)

    def rim(m_ref, e, h):
        build(e, h, 0, -1, X - 1, range(Y + 2))
        spread(m_ref, 0, 0, W, (0,))
        build(e, h, X + 1, 1, 0, range(Y + 2))
        spread(m_ref, X + 1, 0, W, (2,))

        def body(x, carry):
            build(e, h, x + 1, 0, x, (0, Y + 1))
            spread(m_ref, x + 1, 0, L, (0, 1, 2))
            spread(m_ref, x + 1, I1, I1 + L, (0, 1, 2))
            return carry

        lax.fori_loop(0, X, body, 0)

    def clear_pad(ref):
        for x in range(X + 4):
            if x < 2 or x >= X + 2:
                ref[x] = jnp.zeros((2 * C, (Y + 4) * L), BF)
            else:
                ref[x, :, 0 : 2 * L] = jnp.zeros((2 * C, 2 * L), BF)
                ref[x, :, (Y + 2) * L : (Y + 4) * L] = jnp.zeros((2 * C, 2 * L), BF)

    def put_pad(ref, x, v):
        hi, lo = split(v)
        ref[x + 2, 0:C, 2 * L : (Y + 2) * L] = hi
        ref[x + 2, C : 2 * C, 2 * L : (Y + 2) * L] = lo

    def correlate(ref):
        acc_ref[...] = jnp.zeros((2 * ROWS, L), F32)

        def body(xp, carry):
            left = jnp.concatenate(
                [
                    ref[xp - a + 2, :, (2 - b) * L : (2 - b) * L + W]
                    for a in range(3)
                    for b in range(3)
                ],
                axis=0,
            )
            acc_ref[:, 0 : 6 * C] += lax.dot_general(
                left, r_ref[xp], (((1,), (1,)), ((), ())), preferred_element_type=F32
            )
            return carry

        lax.fori_loop(0, X + 2, body, 0)
        pieces = []
        for k in range(9):
            t = acc_ref[2 * k * C : (2 * k + 1) * C] + acc_ref[(2 * k + 1) * C : (2 * k + 2) * C]
            pieces.append(t + pltpu.roll(t, L - 3 * C, 1))
        return pieces

    def put_weights(m_ref, k, t):
        hi = t.astype(BF).astype(F32)
        m_ref[k * C : (k + 1) * C, :] = jnp.concatenate([hi, hi, t - hi], axis=1).astype(BF)

    def weights_forward():
        for k in range(9):
            at = k * 3 * C
            put_weights(
                mf_ref, k,
                jnp.concatenate([wv[at + c * C : at + (c + 1) * C] for c in range(3)], axis=1),
            )

    def weights_backward():
        for k in range(9):
            at = (8 - k) * 3 * C
            put_weights(
                mb_ref, k,
                jnp.concatenate(
                    [wv[at + c * C : at + (c + 1) * C] for c in (2, 1, 0)], axis=0
                ).T,
            )

    def as_column(ref):
        square = lax.broadcasted_iota(jnp.int32, (C, C), 0) == lax.broadcasted_iota(
            jnp.int32, (C, C), 1
        )
        return jnp.sum(jnp.where(square, ref[...], 0.0), axis=1, keepdims=True)

    loads[0].wait()
    bring(vin, ev, cbv)
    pl.semaphore_wait(barrier, greets)
    send_cols(0, cbv)
    send_faces(0, ev)
    for copy in loads[1:]:
        copy.wait()
    clear()
    weights_forward()
    bring(cin, ec, cbc)
    pass_tiles(0, cbv, hv)
    send_cols(1, cbc)
    send_faces(1, ec)
    interior(mf_ref, ev, hv)
    clear_pad(agp)
    clear_pad(cvp)
    weights_backward()

    def vol_sum(x, s):
        return s + jnp.sum(ev[x + 1, :, I0:I1], axis=1, keepdims=True)

    in_sum = lax.fori_loop(0, X, vol_sum, jnp.zeros((C, 1), F32))
    wait_halo(0, ev, hv)
    rim(mf_ref, ev, hv)

    def gather_conv(x, sums):
        s, q = sums
        t = o_ref[x + 2, :, 2 * L : (Y + 2) * L]
        eo[x + 1, :, I0:I1] = t
        return (
            s + jnp.sum(t, axis=1, keepdims=True),
            q + jnp.sum(t * t, axis=1, keepdims=True),
        )

    zero_col = jnp.zeros((C, 1), F32)
    s, q = lax.fori_loop(0, X, gather_conv, (zero_col, zero_col))
    start(s_z1, pack((s, q, in_sum)))
    columns_of(eo, cbo)
    send_cols(2, cbo)

    def pad_conv(x, carry):
        put_pad(cvp, x, eo[x + 1, :, I0:I1])
        return carry

    lax.fori_loop(0, X, pad_conv, 0)
    part = finish(s_z1)
    start(s_p1, part)
    send_faces(2, eo)
    pass_tiles(1, cbc, hc)
    cross = correlate(cvp)
    for k in range(9):
        gw[k * C : (k + 1) * C] = pltpu.roll(cross[k], half, 1)
    pass_tiles(2, cbo, ho)
    clear()
    gain = as_column(gv)
    shift = as_column(bv)
    total1 = finish(s_p1)
    mean = unpack(total1, 0) / count
    var = unpack(total1, 1) / count - mean * mean
    rstd = lax.rsqrt(var + 1e-05)

    def slope(conv, cot):
        normed = (conv - mean) * rstd
        act = gain * normed + shift
        sig = 1.0 / (1.0 + jnp.exp(-act))
        return cot * sig * (1.0 + act * (1.0 - sig)), normed

    def local_slope(x, sums):
        sg, sb = sums
        a, normed = slope(eo[x + 1, :, I0:I1], ec[x + 1, :, I0:I1])
        ea[x + 1, :, I0:I1] = a
        put_pad(agp, x, a)
        return (
            sg + jnp.sum(a * normed, axis=1, keepdims=True),
            sb + jnp.sum(a, axis=1, keepdims=True),
        )

    sg, sb = lax.fori_loop(0, X, local_slope, (zero_col, zero_col))
    start(s_z2, pack((sg, sb)))
    cross = correlate(agp)
    for k in range(9):
        gw[k * C : (k + 1) * C] = jnp.where(lane < half, cross[k], gw[k * C : (k + 1) * C])
    if gw.shape[0] > ROWS:
        gw[ROWS:] = jnp.zeros((gw.shape[0] - ROWS, L), F32)
    chunk = gw.shape[0] // npl

    def piece(j):
        return gw.at[pl.ds(pl.multiple_of(j * chunk, 8), chunk)]

    def scatter(d, arriving=False):
        to = lax.rem(mp + d, npl)
        slot = lax.rem(mp + (npl - d), npl) if arriving else mp
        return pltpu.make_async_remote_copy(
            src_ref=piece(to), dst_ref=gp_buf.at[slot],
            send_sem=gsend.at[0, d], recv_sem=grecv.at[0, d],
            device_id=plane_id(to), device_id_type=MESH,
        )

    part = finish(s_z2)
    start(s_p2, part)
    gp_buf[mp] = gw[pl.ds(pl.multiple_of(mp * chunk, 8), chunk)]
    for d in range(1, npl):
        scatter(d).start()

    wait_halo(1, ec, hc)
    wait_halo(2, eo, ho)
    for xp in (0, X + 1):
        a, _ = slope(eo[xp], ec[xp])
        ea[xp] = a

    def edge_slope(x, carry):
        for at in (0, I1):
            a, _ = slope(eo[x + 1, :, at : at + L], ec[x + 1, :, at : at + L])
            ea[x + 1, :, at : at + L] = a
        return carry

    lax.fori_loop(0, X, edge_slope, 0)

    def tile_slope(k, carry):
        a, _ = slope(ho[k], hc[k])
        ha[k] = a
        return carry

    lax.fori_loop(0, 9, tile_slope, 0)

    total2 = finish(s_p2)
    for d in range(1, npl):
        scatter(d, True).wait_recv()
    gpart = gp_buf[0]
    for j in range(1, npl):
        gpart = gpart + gp_buf[j]
    start(g_y, gpart)
    gain_grad = unpack(total2, 0)
    shift_grad = unpack(total2, 1)
    scale = gain * rstd
    k_conv = -scale * rstd * (gain_grad / count)
    k_one = -scale * (shift_grad / count) - k_conv * mean

    def blend(xp, carry):
        ea[xp] = scale * ea[xp] + k_conv * eo[xp] + k_one
        return carry

    lax.fori_loop(0, X + 2, blend, 0)

    def blend_tile(k, carry):
        ha[k] = scale * ha[k] + k_conv * ho[k] + k_one
        return carry

    lax.fori_loop(0, 9, blend_tile, 0)
    interior(mb_ref, ea, ha)
    gpart = finish(g_y)
    start(g_f, gpart)
    rim(mb_ref, ea, ha)

    def emit(x, carry):
        for y in range(Y):
            out_ref[pl.ds(x * Y + y, C, stride=X * Y), :] = o_ref[
                x + 2, :, (y + 2) * L : (y + 3) * L
            ]
        return carry

    lax.fori_loop(0, X, emit, 0)
    gout_ref[...] = total2[:, 0:C]
    bout_ref[...] = pltpu.roll(total2, L - C, 1)[:, 0:C]
    wide = jnp.sum(
        jnp.where(lax.rem(lane, C) == sub, unpack(total1, 2), 0.0), axis=0, keepdims=True
    )
    arrive(*g_f)
    for j in range(npl):
        gfull[j * chunk : (j + 1) * chunk] = gf_buf[j]
    for k in range(9):
        t = gfull[k * C : (k + 1) * C]
        norm = rstd * (pltpu.roll(t, half, 1) - mean * wide)
        t = scale * (t - (shift_grad / count) * wide - (gain_grad / count) * norm)
        for c in range(3):
            at = (k * 3 + c) * C
            wout_ref[at : at + C, :] = (t if c == 0 else pltpu.roll(t, L - c * C, 1))[:, 0:C]

    drain_halo(0, ev, cbv, hv)
    drain_halo(1, ec, cbc, hc)
    drain_halo(2, eo, cbo, ho)
    for spec in (s_z1, s_p1, s_z2, s_p2, g_y, g_f):
        settle(spec)
    for d in range(1, npl):
        scatter(d).wait_send()


def shards(sizes, volume, weight, gamma, beta, cotangent):
    nx, ny, nz = sizes
    _, X, Y, Z = volume.shape
    count = float(X * Y * Z * nx * ny * nz)
    W = (Y + 2) * L
    npl = nx * nz
    chunk = -(-(ROWS // 8) // npl) * 8
    rows = chunk * npl
    vmem = pl.BlockSpec(memory_space=pltpu.VMEM)
    hbm = pl.BlockSpec(memory_space=pl.ANY)
    e_shape = pltpu.VMEM((X + 2, C, W), F32)
    h_shape = pltpu.VMEM((9, C, L), F32)
    cb_shape = pltpu.VMEM((4, C, L), F32)
    pad_shape = pltpu.VMEM((X + 4, 2 * C, (Y + 4) * L), BF)
    m_shape = pltpu.VMEM((ROWS, ROWS), BF)
    line_rows = pltpu.VMEM((ny, 1, L), F32)
    plane_rows = pltpu.VMEM((npl, 1, L), F32)
    dma = pltpu.SemaphoreType.DMA
    most = max(npl, ny)
    flat, wflat, gain_grad, shift_grad = pl.pallas_call(
        functools.partial(kernel, (nx, ny, nz, X, Y), count),
        out_shape=(
            jax.ShapeDtypeStruct((C * X * Y, L), F32),
            jax.ShapeDtypeStruct((27 * C, C), F32),
            jax.ShapeDtypeStruct((1, C), F32),
            jax.ShapeDtypeStruct((1, C), F32),
        ),
        in_specs=[hbm, hbm, hbm, hbm, hbm],
        out_specs=(vmem, vmem, vmem, vmem),
        scratch_shapes=[
            pltpu.VMEM((C * X * Y, L), F32), pltpu.VMEM((C * X * Y, L), F32),
            pltpu.VMEM((27 * C, C), F32), pltpu.VMEM((1, C), F32), pltpu.VMEM((1, C), F32),
            m_shape, m_shape,
            e_shape, e_shape, e_shape, e_shape,
            h_shape, h_shape, h_shape, h_shape,
            cb_shape, cb_shape, cb_shape,
            pltpu.VMEM((X + 2, 6 * C, W), BF),
            pltpu.VMEM((X + 4, C, (Y + 4) * L), F32),
            pad_shape, pad_shape,
            pltpu.VMEM((2 * ROWS, L), F32),
            pltpu.VMEM((rows, L), F32), pltpu.VMEM((rows, L), F32),
            line_rows, plane_rows, line_rows, plane_rows,
            pltpu.VMEM((npl, chunk, L), F32), pltpu.VMEM((ny, chunk, L), F32),
            pltpu.VMEM((npl, chunk, L), F32),
            dma((5,)), dma((3, 18)), dma((3, 18)), dma((4, most)), dma((4, most)),
            dma((3, most)), dma((3, most)),
        ],
        compiler_params=pltpu.CompilerParams(
            collective_id=0, has_side_effects=True, vmem_limit_bytes=60 << 20
        ),
    )(
        volume.reshape(C * X * Y, L), cotangent.reshape(C * X * Y, L),
        weight.transpose(2, 3, 4, 0, 1).reshape(27 * C, C),
        gamma.reshape(1, C), beta.reshape(1, C),
    )
    return (
        flat.reshape(C, X, Y, Z),
        wflat.reshape(3, 3, 3, C, C).transpose(3, 4, 0, 1, 2),
        gain_grad.reshape(C),
        shift_grad.reshape(C),
    )


def solution(mesh):
    sizes = tuple(mesh.shape[name] for name in ("gx", "gy", "gz"))
    spec = P(None, "gx", "gy", "gz")
    return jax.shard_map(
        functools.partial(shards, sizes),
        mesh=mesh,
        in_specs=(spec, P(), P(), P(), spec),
        out_specs=(spec, P(), P(), P()),
        check_vma=False,
    )
```

time: 76.7 us -> 66.7 us (0.87)
  local copies, waits for them, and re-layouts: 8.39 us -> 3.79 us
  Pallas kernels: 64.9 us -> 62.1 us
  other arithmetic: 2.38 us -> 0 us
    pallas_call x1, Pallas kernels: 64.9 us -> 62.1 us  [shards(): pl.pallas_call(functools.partial(kernel, (nx, ny, nz, X, Y), count), out_...]
    reshape x8 -> x0, local copies, waits for them, and re-layouts: 2.19 us -> none  [the longest x1 0.68 us: shards(): gamma.reshape(C, 1)]
    transpose x4 -> x0, local copies, waits for them, and re-layouts: 2.07 us -> none  [the longest x2 1.07 us: shards(): weight[:, :, ::-1, ::-1, ::-1].transpose(2, 3, 1, 4, 0).reshape(ROWS, 3 * C)]
    div x2 -> x0, other arithmetic: 1.18 us -> none  [the longest x1 0.59 us: shards(): beta_grad / count]
    concatenate x2 -> x0, other arithmetic: 0.89 us -> none  [the longest x1 0.81 us: stack(): return jnp.concatenate([hi, hi, lo], axis=1).astype(BF)]
where the time goes in v1:
time: 66.7 us; the launch traced here: 66.6 us
  Pallas kernels  62.1 us (93%)
  local copies, waits for them, and re-layouts  3.79 us (6%)
    pallas_call x1, Pallas kernels, shards(): pl.pallas_call(functools.partial(kernel, (nx, ny, nz, X, Y), count), out_...  62.1 us
    unnamed x10, local copies, waits for them, and re-layouts  3.79 us

profile of v1, /device:TPU:1, one launch (start us, length us, event | category | flops | bytes accessed | tf_op | source)
XLA Modules:
  0.0 66.6 jit_solution(10337872333587449256)
XLA Ops:
  0.6 62.1 %shard_map.84 = (f32[1024,128]{1,0:T(8,128)}, f32[432,16]{1,0:T(8,128)}, f32[1,16]{1,0:T(1,128)}, f32[1,16]{1,0:T(1,128)}) custom-call(f32[1024,128]{1,0:T(8,128)} %bitcast.13, f32[1024,128]{1,0:T(8,128)} %bitcast.14, f32[432,16]{1,0:T(8,128)} %bitcast.17, f32[1,16]{1,0:T(1,128)} %bitcast.18, f32[1,16]{1,0:T(1,128)} %bitcast.19), custom_call_target="tpu_custom_call" | custom-call | tf_op jit(solution)/shard_map/pallas_call | solution.py:551
  62.8 0.0 copy-start
  62.8 1.9 %copy.13 = f32[16,4,16,128]{3,2,1,0:T(8,128)} copy(f32[16,4,16,128]{3,2,1,0:T(8,128)} %bitcast.15) | data formatting | bytes 1048576
  64.7 0.0 copy-done
  64.7 0.0 copy-start.2
  64.7 0.7 %copy.14 = f32[16,16,3,3,3]{1,0,4,3,2:T(8,128)} copy(f32[16,16,3,3,3]{1,0,4,3,2:T(8,128)S(1)} %bitcast.16) | data formatting | bytes 55296
  65.4 0.0 copy-done.2
  65.4 0.0 copy-start.1
  65.4 0.5 copy.15
  65.9 0.2 copy-done.1
  66.1 0.5 copy.16
Async XLA Ops:
  62.8 1.9 %copy-start = (f32[432,16]{1,0:T(8,128)S(1)}, f32[432,16]{1,0:T(8,128)}, u32[]{:S(2)}) copy-start(f32[432,16]{1,0:T(8,128)} %get-tuple-element.9) | copy-start | bytes 82948
  64.7 0.7 %copy-start.2 = (f32[1,16]{1,0:T(1,128)S(1)}, f32[1,16]{1,0:T(1,128)}, u32[]{:S(2)}) copy-start(f32[1,16]{1,0:T(1,128)} %get-tuple-element.10) | copy-start | bytes 196
  65.4 0.7 %copy-start.1 = (f32[1,16]{1,0:T(1,128)S(1)}, f32[1,16]{1,0:T(1,128)}, u32[]{:S(2)}) copy-start(f32[1,16]{1,0:T(1,128)} %get-tuple-element.11) | copy-start | bytes 196

commit v2 on v1

--- a/solution.py
+++ b/solution.py
@@ -38,26 +38,31 @@
     sub = lax.broadcasted_iota(jnp.int32, (C, L), 0)
     half = L // 2
     npl = nx * nz
-    mp = mx * nz + mz
-
-    def plane_id(q):
-        return {"gx": lax.div(q, nz), "gz": lax.rem(q, nz)}
-
-    def line_id(q):
-        return {"gy": q}
-
-    plane = (plane_id, mp, npl)
-    line = (line_id, my, ny)
-
-    def near(m, s, n):
-        return lax.rem(m + (s + n), n)
+    xs_at = [mx] + [lax.rem(mx + d, nx) for d in range(1, nx)]
+    ys_at = [my] + [lax.rem(my + d, ny) for d in range(1, ny)]
+    zs_at = [mz] + [lax.rem(mz + d, nz) for d in range(1, nz)]
+    xs_row = [x * nz for x in xs_at]
+    mp = xs_row[0] + mz
+    plane = (
+        mp, npl,
+        [
+            (
+                dx * nz + dz, {"gx": xs_at[dx], "gz": zs_at[dz]},
+                xs_row[dx] + zs_at[dz], xs_row[-dx] + zs_at[-dz],
+            )
+            for dx in range(nx)
+            for dz in range(nz)
+            if dx or dz
+        ],
+    )
+    line = (my, ny, [(d, {"gy": ys_at[d]}, ys_at[d], ys_at[-d]) for d in range(1, ny)])
 
     def side_id(sx, sy):
         out = {}
         if sx:
-            out["gx"] = near(mx, sx, nx)
+            out["gx"] = xs_at[sx]
         if sy:
-            out["gy"] = near(my, sy, ny)
+            out["gy"] = ys_at[sy]
         return out
 
     loads = [
@@ -71,11 +76,9 @@
 
     barrier = pltpu.get_barrier_semaphore()
     greets = 0
-    for name, m, n in (plane, line):
-        for d in range(1, n):
-            pl.semaphore_signal(
-                barrier, inc=1, device_id=name(lax.rem(m + d, n)), device_id_type=MESH
-            )
+    for group in (plane, line):
+        for _, there, _, _ in group[2]:
+            pl.semaphore_signal(barrier, inc=1, device_id=there, device_id_type=MESH)
             greets += 1
     for sx, sy in SIDES:
         if sx and sy:
@@ -102,7 +105,7 @@
         return pltpu.make_async_remote_copy(
             src_ref=cb.at[k], dst_ref=cb.at[2 + k],
             send_sem=hsend.at[which, 8 + k], recv_sem=hrecv.at[which, 8 + k],
-            device_id={"gz": near(mz, s, nz)}, device_id_type=MESH,
+            device_id={"gz": zs_at[s]}, device_id_type=MESH,
         )
 
     def tile_copy(which, h, k):
@@ -142,33 +145,39 @@
         for k in range(8):
             tile_copy(which, h, k).wait_send()
 
-    def peer(buf, group, ss, rs, d, arriving=False):
-        name, m, n = group
-        slot = lax.rem(m + (n - d), n) if arriving else m
+    def peer(buf, group, ss, rs, one, arriving=False):
+        k, there, _, opposite = one
+        own = group[0]
         return pltpu.make_async_remote_copy(
-            src_ref=buf.at[m], dst_ref=buf.at[slot], send_sem=ss.at[d], recv_sem=rs.at[d],
-            device_id=name(lax.rem(m + d, n)), device_id_type=MESH,
+            src_ref=buf.at[own], dst_ref=buf.at[opposite if arriving else own],
+            send_sem=ss.at[k], recv_sem=rs.at[k], device_id=there, device_id_type=MESH,
         )
 
     def arrive(buf, group, ss, rs):
-        for d in range(1, group[2]):
-            peer(buf, group, ss, rs, d, True).wait_recv()
+        for one in group[2]:
+            peer(buf, group, ss, rs, one, True).wait_recv()
 
     def start(spec, value):
-        spec[0][spec[1][1]] = value
-        for d in range(1, spec[1][2]):
-            peer(*spec, d).start()
+        spec[0][spec[1][0]] = value
+        for one in spec[1][2]:
+            peer(*spec, one).start()
+
+    def slots(buf, n):
+        total = [buf[j] for j in range(n)]
+        while len(total) > 1:
+            total = [
+                total[j] + total[j + 1] if j + 1 < len(total) else total[j]
+                for j in range(0, len(total), 2)
+            ]
+        return total[0]
 
     def finish(spec):
         arrive(*spec)
-        total = spec[0][0]
-        for j in range(1, spec[1][2]):
-            total = total + spec[0][j]
-        return total
+        return slots(spec[0], spec[1][1])
 
     def settle(spec):
-        for d in range(1, spec[1][2]):
-            peer(*spec, d).wait_send()
+        for one in spec[1][2]:
+            peer(*spec, one).wait_send()
 
     s_z1 = (z1, line, asend.at[0], arecv.at[0])
     s_p1 = (p1, plane, asend.at[1], arecv.at[1])
@@ -431,20 +440,17 @@
     def piece(j):
         return gw.at[pl.ds(pl.multiple_of(j * chunk, 8), chunk)]
 
-    def scatter(d, arriving=False):
-        to = lax.rem(mp + d, npl)
-        slot = lax.rem(mp + (npl - d), npl) if arriving else mp
+    def scatter(one, arriving=False):
+        k, there, to, opposite = one
         return pltpu.make_async_remote_copy(
-            src_ref=piece(to), dst_ref=gp_buf.at[slot],
-            send_sem=gsend.at[0, d], recv_sem=grecv.at[0, d],
-            device_id=plane_id(to), device_id_type=MESH,
-        )
-
-    part = finish(s_z2)
-    start(s_p2, part)
+            src_ref=piece(to), dst_ref=gp_buf.at[opposite if arriving else mp],
+            send_sem=gsend.at[0, k], recv_sem=grecv.at[0, k],
+            device_id=there, device_id_type=MESH,
+        )
+
     gp_buf[mp] = gw[pl.ds(pl.multiple_of(mp * chunk, 8), chunk)]
-    for d in range(1, npl):
-        scatter(d).start()
+    for one in plane[2]:
+        scatter(one).start()
 
     wait_halo(1, ec, hc)
     wait_halo(2, eo, ho)
@@ -467,13 +473,12 @@
 
     lax.fori_loop(0, 9, tile_slope, 0)
 
+    part = finish(s_z2)
+    start(s_p2, part)
+    for one in plane[2]:
+        scatter(one, True).wait_recv()
+    start(g_y, slots(gp_buf, npl))
     total2 = finish(s_p2)
-    for d in range(1, npl):
-        scatter(d, True).wait_recv()
-    gpart = gp_buf[0]
-    for j in range(1, npl):
-        gpart = gpart + gp_buf[j]
-    start(g_y, gpart)
     gain_grad = unpack(total2, 0)
     shift_grad = unpack(total2, 1)
     scale = gain * rstd
@@ -525,8 +530,20 @@
     drain_halo(2, eo, cbo, ho)
     for spec in (s_z1, s_p1, s_z2, s_p2, g_y, g_f):
         settle(spec)
-    for d in range(1, npl):
-        scatter(d).wait_send()
+    for one in plane[2]:
+        scatter(one).wait_send()
+
+
+def store(*refs):
+    n = len(refs) // 2
+    sem = refs[-1]
+    copies = [
+        pltpu.make_async_copy(refs[k], refs[n + k], sem.at[k]) for k in range(n)
+    ]
+    for copy in copies:
+        copy.start()
+    for copy in copies:
+        copy.wait()
 
 
 def shards(sizes, volume, weight, gamma, beta, cotangent):
@@ -538,7 +555,6 @@
     chunk = -(-(ROWS // 8) // npl) * 8
     rows = chunk * npl
     vmem = pl.BlockSpec(memory_space=pltpu.VMEM)
-    hbm = pl.BlockSpec(memory_space=pl.ANY)
     e_shape = pltpu.VMEM((X + 2, C, W), F32)
     h_shape = pltpu.VMEM((9, C, L), F32)
     cb_shape = pltpu.VMEM((4, C, L), F32)
@@ -548,15 +564,16 @@
     plane_rows = pltpu.VMEM((npl, 1, L), F32)
     dma = pltpu.SemaphoreType.DMA
     most = max(npl, ny)
-    flat, wflat, gain_grad, shift_grad = pl.pallas_call(
+    results = (
+        jax.ShapeDtypeStruct((C * X * Y, L), F32),
+        jax.ShapeDtypeStruct((27 * C, C), F32),
+        jax.ShapeDtypeStruct((1, C), F32),
+        jax.ShapeDtypeStruct((1, C), F32),
+    )
+    made = pl.pallas_call(
         functools.partial(kernel, (nx, ny, nz, X, Y), count),
-        out_shape=(
-            jax.ShapeDtypeStruct((C * X * Y, L), F32),
-            jax.ShapeDtypeStruct((27 * C, C), F32),
-            jax.ShapeDtypeStruct((1, C), F32),
-            jax.ShapeDtypeStruct((1, C), F32),
-        ),
-        in_specs=[hbm, hbm, hbm, hbm, hbm],
+        out_shape=results,
+        in_specs=[pl.BlockSpec(memory_space=pltpu.HBM)] * 5,
         out_specs=(vmem, vmem, vmem, vmem),
         scratch_shapes=[
             pltpu.VMEM((C * X * Y, L), F32), pltpu.VMEM((C * X * Y, L), F32),
@@ -577,13 +594,26 @@
             dma((3, most)), dma((3, most)),
         ],
         compiler_params=pltpu.CompilerParams(
-            collective_id=0, has_side_effects=True, vmem_limit_bytes=60 << 20
+            collective_id=0, has_side_effects=True, vmem_limit_bytes=24 << 20
         ),
     )(
-        volume.reshape(C * X * Y, L), cotangent.reshape(C * X * Y, L),
-        weight.transpose(2, 3, 4, 0, 1).reshape(27 * C, C),
-        gamma.reshape(1, C), beta.reshape(1, C),
+        *(
+            pltpu.with_memory_space_constraint(v, pltpu.HBM)
+            for v in (
+                volume.reshape(C * X * Y, L), cotangent.reshape(C * X * Y, L),
+                weight.transpose(2, 3, 4, 0, 1).reshape(27 * C, C),
+                gamma.reshape(1, C), beta.reshape(1, C),
+            )
+        )
     )
+    flat, wflat, gain_grad, shift_grad = pl.pallas_call(
+        store,
+        out_shape=results,
+        in_specs=[vmem] * 4,
+        out_specs=[pl.BlockSpec(memory_space=pltpu.HBM)] * 4,
+        scratch_shapes=[dma((4,))],
+        compiler_params=pltpu.CompilerParams(vmem_limit_bytes=8 << 20),
+    )(*made)
     return (
         flat.reshape(C, X, Y, Z),
         wflat.reshape(3, 3, 3, C, C).transpose(3, 4, 0, 1, 2),

time: 66.7 us -> 60 us (0.90)
  local copies, waits for them, and re-layouts: 3.79 us -> 0 us
  Pallas kernels: 62.1 us -> 59.2 us
    pallas_call x1, Pallas kernels: 62.1 us -> 58.3 us  [shards(): pl.pallas_call(functools.partial(kernel, (nx, ny, nz, X, Y), count), out_...]
    unnamed x10 -> x0, local copies, waits for them, and re-layouts: 3.79 us -> none
    pallas_call x0 -> x1, Pallas kernels: none -> 0.9 us  [shards(): pl.pallas_call(store, out_shape=results, in_specs=[vmem] * 4, out_specs=[...]
where the time goes in v2:
time: 60 us; the launch traced here: 59.9 us
  Pallas kernels  59.2 us (99%)
  between operations  0.64 us (1%)
    pallas_call x1, Pallas kernels, shards(): pl.pallas_call(functools.partial(kernel, (nx, ny, nz, X, Y), count), out_...  58.3 us

profile of v2, /device:TPU:1, one launch (start us, length us, event | category | flops | bytes accessed | tf_op | source)
XLA Modules:
  0.0 59.9 jit_solution(3956116431061938766)
XLA Ops:
  0.6 58.3 %shard_map.84 = (f32[1024,128]{1,0:T(8,128)S(1)}, f32[432,16]{1,0:T(8,128)S(1)}, f32[1,16]{1,0:T(1,128)S(1)}, f32[1,16]{1,0:T(1,128)S(1)}) custom-call(f32[1024,128]{1,0:T(8,128)} %bitcast.13, f32[1024,128]{1,0:T(8,128)} %bitcast.14, f32[432,16]{1,0:T(8,128)} %bitcast.15, f32[1,16]{1,0:T(1,128)} %bitcast.16, f32[1,16]{1,0:T(1,128)} %bitcast.17), custom_call_target="tpu_custom_call" | custom-call | tf_op jit(solution)/shard_map/pallas_call | solution.py:573
  59.0 0.9 %shard_map.85 = (f32[1024,128]{1,0:T(8,128)}, f32[432,16]{1,0:T(8,128)}, f32[1,16]{1,0:T(1,128)}, f32[1,16]{1,0:T(1,128)}) custom-call(f32[1024,128]{1,0:T(8,128)S(1)} %get-tuple-element.12.refs_0_, f32[432,16]{1,0:T(8,128)S(1)} %get-tuple-element.13.refs_1_, f32[1,16]{1,0:T(1,128)S(1)} %get-tuple-element.14.refs_2_, f32[1,16]{1,0:T(1,128)S(1)} %get-tuple-element.15.refs_3_), custom_call_target="tpu_custom_call" | custom-call | tf_op jit(solution)/shard_map/pallas_call | solution.py:609

commit v3 on v2

--- a/solution.py
+++ b/solution.py
@@ -46,16 +46,13 @@
     plane = (
         mp, npl,
         [
-            (
-                dx * nz + dz, {"gx": xs_at[dx], "gz": zs_at[dz]},
-                xs_row[dx] + zs_at[dz], xs_row[-dx] + zs_at[-dz],
-            )
+            ({"gx": xs_at[dx], "gz": zs_at[dz]}, xs_row[dx] + zs_at[dz])
             for dx in range(nx)
             for dz in range(nz)
             if dx or dz
         ],
     )
-    line = (my, ny, [(d, {"gy": ys_at[d]}, ys_at[d], ys_at[-d]) for d in range(1, ny)])
+    line = (my, ny, [({"gy": ys_at[d]}, ys_at[d]) for d in range(1, ny)])
 
     def side_id(sx, sy):
         out = {}
@@ -77,7 +74,7 @@
     barrier = pltpu.get_barrier_semaphore()
     greets = 0
     for group in (plane, line):
-        for _, there, _, _ in group[2]:
+        for there, _ in group[2]:
             pl.semaphore_signal(barrier, inc=1, device_id=there, device_id_type=MESH)
             greets += 1
     for sx, sy in SIDES:
@@ -92,11 +89,15 @@
         dst_y = {1: pl.ds(0, L), -1: pl.ds(I1, L), 0: pl.ds(I0, Y * L)}[sy]
         return ref.at[src_x, :, src_y], ref.at[dst_x, :, dst_y]
 
+    def await_bytes(ref, sem):
+        pltpu.make_async_copy(ref, ref, sem).wait()
+
     def face_copy(which, ref, k):
         sx, sy = SIDES[k]
         src, dst = face(ref, sx, sy)
+        kind = 2 if sx and sy else (0 if sx else 1)
         return pltpu.make_async_remote_copy(
-            src_ref=src, dst_ref=dst, send_sem=hsend.at[which, k], recv_sem=hrecv.at[which, k],
+            src_ref=src, dst_ref=dst, send_sem=hsend.at[which, kind], recv_sem=hrecv.at[which, kind],
             device_id=side_id(sx, sy), device_id_type=MESH,
         )
 
@@ -104,7 +105,7 @@
         s = 1 - 2 * k
         return pltpu.make_async_remote_copy(
             src_ref=cb.at[k], dst_ref=cb.at[2 + k],
-            send_sem=hsend.at[which, 8 + k], recv_sem=hrecv.at[which, 8 + k],
+            send_sem=hsend.at[which, 3], recv_sem=hrecv.at[which, 3],
             device_id={"gz": zs_at[s]}, device_id_type=MESH,
         )
 
@@ -112,7 +113,7 @@
         sx, sy = SIDES[k]
         return pltpu.make_async_remote_copy(
             src_ref=h.at[4], dst_ref=h.at[(1 - sx) * 3 + (1 - sy)],
-            send_sem=hsend.at[which, 10 + k], recv_sem=hrecv.at[which, 10 + k],
+            send_sem=hsend.at[which, 4], recv_sem=hrecv.at[which, 4],
             device_id=side_id(sx, sy), device_id_type=MESH,
         )
 
@@ -125,37 +126,33 @@
             face_copy(which, e, k).start()
 
     def pass_tiles(which, cb, h):
-        for k in range(2):
-            col_copy(which, cb, k).wait_recv()
+        await_bytes(cb.at[pl.ds(2, 2)], hrecv.at[which, 3])
         h[4] = jnp.where(lane < half, cb[2], cb[3])
         for k in range(8):
             tile_copy(which, h, k).start()
 
+    def faces_done(e, h, sems):
+        await_bytes(e.at[pl.ds(0, 2), :, pl.ds(I0, Y * L)], sems.at[0])
+        await_bytes(e.at[pl.ds(1, X), :, pl.ds(0, 2 * L)], sems.at[1])
+        await_bytes(e.at[0, :, pl.ds(0, 4 * L)], sems.at[2])
+        await_bytes(h.at[pl.ds(0, 8)], sems.at[4])
+
     def wait_halo(which, e, h):
-        for k in range(8):
-            face_copy(which, e, k).wait_recv()
-        for k in range(8):
-            tile_copy(which, h, k).wait_recv()
+        faces_done(e, h, hrecv.at[which])
 
     def drain_halo(which, e, cb, h):
-        for k in range(8):
-            face_copy(which, e, k).wait_send()
-        for k in range(2):
-            col_copy(which, cb, k).wait_send()
-        for k in range(8):
-            tile_copy(which, h, k).wait_send()
-
-    def peer(buf, group, ss, rs, one, arriving=False):
-        k, there, _, opposite = one
-        own = group[0]
+        faces_done(e, h, hsend.at[which])
+        await_bytes(cb.at[pl.ds(0, 2)], hsend.at[which, 3])
+
+    def peer(buf, group, ss, rs, one):
+        there, own = one[0], group[0]
         return pltpu.make_async_remote_copy(
-            src_ref=buf.at[own], dst_ref=buf.at[opposite if arriving else own],
-            send_sem=ss.at[k], recv_sem=rs.at[k], device_id=there, device_id_type=MESH,
+            src_ref=buf.at[own], dst_ref=buf.at[own], send_sem=ss, recv_sem=rs,
+            device_id=there, device_id_type=MESH,
         )
 
     def arrive(buf, group, ss, rs):
-        for one in group[2]:
-            peer(buf, group, ss, rs, one, True).wait_recv()
+        await_bytes(buf.at[pl.ds(0, group[1] - 1)], rs)
 
     def start(spec, value):
         spec[0][spec[1][0]] = value
@@ -176,8 +173,7 @@
         return slots(spec[0], spec[1][1])
 
     def settle(spec):
-        for one in spec[1][2]:
-            peer(*spec, one).wait_send()
+        await_bytes(spec[0].at[pl.ds(0, spec[1][1] - 1)], spec[2])
 
     s_z1 = (z1, line, asend.at[0], arecv.at[0])
     s_p1 = (p1, plane, asend.at[1], arecv.at[1])
@@ -440,11 +436,10 @@
     def piece(j):
         return gw.at[pl.ds(pl.multiple_of(j * chunk, 8), chunk)]
 
-    def scatter(one, arriving=False):
-        k, there, to, opposite = one
+    def scatter(one):
+        there, to = one
         return pltpu.make_async_remote_copy(
-            src_ref=piece(to), dst_ref=gp_buf.at[opposite if arriving else mp],
-            send_sem=gsend.at[0, k], recv_sem=grecv.at[0, k],
+            src_ref=piece(to), dst_ref=gp_buf.at[mp], send_sem=gsend.at[0], recv_sem=grecv.at[0],
             device_id=there, device_id_type=MESH,
         )
 
@@ -475,8 +470,7 @@
 
     part = finish(s_z2)
     start(s_p2, part)
-    for one in plane[2]:
-        scatter(one, True).wait_recv()
+    await_bytes(gp_buf.at[pl.ds(0, npl - 1)], grecv.at[0])
     start(g_y, slots(gp_buf, npl))
     total2 = finish(s_p2)
     gain_grad = unpack(total2, 0)
@@ -514,24 +508,28 @@
     wide = jnp.sum(
         jnp.where(lax.rem(lane, C) == sub, unpack(total1, 2), 0.0), axis=0, keepdims=True
     )
+    k_norm = scale * rstd * (gain_grad / count)
+    k_wide = (k_norm * mean - scale * (shift_grad / count)) * wide
+    drain_halo(0, ev, cbv, hv)
+    drain_halo(1, ec, cbc, hc)
+    drain_halo(2, eo, cbo, ho)
+    for spec in (s_z1, s_p1, s_z2, s_p2, g_y):
+        settle(spec)
+    await_bytes(gp_buf.at[pl.ds(0, npl - 1)], gsend.at[0])
     arrive(*g_f)
-    for j in range(npl):
-        gfull[j * chunk : (j + 1) * chunk] = gf_buf[j]
+    if chunk != 8:
+        for j in range(npl):
+            gfull[j * chunk : (j + 1) * chunk] = gf_buf[j]
     for k in range(9):
-        t = gfull[k * C : (k + 1) * C]
-        norm = rstd * (pltpu.roll(t, half, 1) - mean * wide)
-        t = scale * (t - (shift_grad / count) * wide - (gain_grad / count) * norm)
+        if chunk == 8:
+            t = jnp.concatenate([gf_buf[2 * k], gf_buf[2 * k + 1]], axis=0)
+        else:
+            t = gfull[k * C : (k + 1) * C]
+        t = scale * t - k_norm * pltpu.roll(t, half, 1) + k_wide
         for c in range(3):
             at = (k * 3 + c) * C
             wout_ref[at : at + C, :] = (t if c == 0 else pltpu.roll(t, L - c * C, 1))[:, 0:C]
-
-    drain_halo(0, ev, cbv, hv)
-    drain_halo(1, ec, cbc, hc)
-    drain_halo(2, eo, cbo, ho)
-    for spec in (s_z1, s_p1, s_z2, s_p2, g_y, g_f):
-        settle(spec)
-    for one in plane[2]:
-        scatter(one).wait_send()
+    settle(g_f)
 
 
 def store(*refs):
@@ -563,7 +561,6 @@
     line_rows = pltpu.VMEM((ny, 1, L), F32)
     plane_rows = pltpu.VMEM((npl, 1, L), F32)
     dma = pltpu.SemaphoreType.DMA
-    most = max(npl, ny)
     results = (
         jax.ShapeDtypeStruct((C * X * Y, L), F32),
         jax.ShapeDtypeStruct((27 * C, C), F32),
@@ -590,8 +587,7 @@
             line_rows, plane_rows, line_rows, plane_rows,
             pltpu.VMEM((npl, chunk, L), F32), pltpu.VMEM((ny, chunk, L), F32),
             pltpu.VMEM((npl, chunk, L), F32),
-            dma((5,)), dma((3, 18)), dma((3, 18)), dma((4, most)), dma((4, most)),
-            dma((3, most)), dma((3, most)),
+            dma((5,)), dma((3, 5)), dma((3, 5)), dma((4,)), dma((4,)), dma((3,)), dma((3,)),
         ],
         compiler_params=pltpu.CompilerParams(
             collective_id=0, has_side_effects=True, vmem_limit_bytes=24 << 20

time: 60 us -> 55 us (0.917)
  Pallas kernels: 59.2 us -> 54.2 us
    pallas_call x1, Pallas kernels: 58.3 us -> 53.3 us  [shards(): pl.pallas_call(functools.partial(kernel, (nx, ny, nz, X, Y), count), out_...]
where the time goes in v3:
time: 55 us; the launch traced here: 54.8 us
  Pallas kernels  54.2 us (99%)
  between operations  0.64 us (1%)
    pallas_call x1, Pallas kernels, shards(): pl.pallas_call(functools.partial(kernel, (nx, ny, nz, X, Y), count), out_...  53.3 us

profile of v3, /device:TPU:1, one launch (start us, length us, event | category | flops | bytes accessed | tf_op | source)
XLA Modules:
  0.0 54.8 jit_solution(6976242861408075617)
XLA Ops:
  0.6 53.3 %shard_map.84 = (f32[1024,128]{1,0:T(8,128)S(1)}, f32[432,16]{1,0:T(8,128)S(1)}, f32[1,16]{1,0:T(1,128)S(1)}, f32[1,16]{1,0:T(1,128)S(1)}) custom-call(f32[1024,128]{1,0:T(8,128)} %bitcast.13, f32[1024,128]{1,0:T(8,128)} %bitcast.14, f32[432,16]{1,0:T(8,128)} %bitcast.15, f32[1,16]{1,0:T(1,128)} %bitcast.16, f32[1,16]{1,0:T(1,128)} %bitcast.17), custom_call_target="tpu_custom_call" | custom-call | tf_op jit(solution)/shard_map/pallas_call | solution.py:570
  53.9 0.9 %shard_map.85 = (f32[1024,128]{1,0:T(8,128)}, f32[432,16]{1,0:T(8,128)}, f32[1,16]{1,0:T(1,128)}, f32[1,16]{1,0:T(1,128)}) custom-call(f32[1024,128]{1,0:T(8,128)S(1)} %get-tuple-element.12.refs_0_, f32[432,16]{1,0:T(8,128)S(1)} %get-tuple-element.13.refs_1_, f32[1,16]{1,0:T(1,128)S(1)} %get-tuple-element.14.refs_2_, f32[1,16]{1,0:T(1,128)S(1)} %get-tuple-element.15.refs_3_), custom_call_target="tpu_custom_call" | custom-call | tf_op jit(solution)/shard_map/pallas_call | solution.py:605

commit v4 on v3

--- a/solution.py
+++ b/solution.py
@@ -111,9 +111,10 @@
 
     def tile_copy(which, h, k):
         sx, sy = SIDES[k]
+        kind = 4 if sx else 5
         return pltpu.make_async_remote_copy(
             src_ref=h.at[4], dst_ref=h.at[(1 - sx) * 3 + (1 - sy)],
-            send_sem=hsend.at[which, 4], recv_sem=hrecv.at[which, 4],
+            send_sem=hsend.at[which, kind], recv_sem=hrecv.at[which, kind],
             device_id=side_id(sx, sy), device_id_type=MESH,
         )
 
@@ -131,17 +132,28 @@
         for k in range(8):
             tile_copy(which, h, k).start()
 
-    def faces_done(e, h, sems):
+    def edges_done(e, h, sems):
+        await_bytes(e.at[pl.ds(1, X), :, pl.ds(0, 2 * L)], sems.at[1])
+        await_bytes(h.at[pl.ds(0, 2)], sems.at[5])
+
+    def sides_done(e, h, sems):
         await_bytes(e.at[pl.ds(0, 2), :, pl.ds(I0, Y * L)], sems.at[0])
-        await_bytes(e.at[pl.ds(1, X), :, pl.ds(0, 2 * L)], sems.at[1])
         await_bytes(e.at[0, :, pl.ds(0, 4 * L)], sems.at[2])
-        await_bytes(h.at[pl.ds(0, 8)], sems.at[4])
+        await_bytes(h.at[pl.ds(0, 6)], sems.at[4])
+
+    def wait_edges(which, e, h):
+        edges_done(e, h, hrecv.at[which])
+
+    def wait_sides(which, e, h):
+        sides_done(e, h, hrecv.at[which])
 
     def wait_halo(which, e, h):
-        faces_done(e, h, hrecv.at[which])
+        wait_edges(which, e, h)
+        wait_sides(which, e, h)
 
     def drain_halo(which, e, cb, h):
-        faces_done(e, h, hsend.at[which])
+        edges_done(e, h, hsend.at[which])
+        sides_done(e, h, hsend.at[which])
         await_bytes(cb.at[pl.ds(0, 2)], hsend.at[which, 3])
 
     def peer(buf, group, ss, rs, one):
@@ -268,51 +280,47 @@
 
         lax.fori_loop(0, X, body, 0)
 
+    def edges(m_ref, e, h):
+        def body(x, carry):
+            build(e, h, x + 1, 0, x, (0, Y + 1))
+            spread(m_ref, x + 1, 0, L, (0, 1, 2))
+            spread(m_ref, x + 1, I1, I1 + L, (0, 1, 2))
+            return carry
+
+        lax.fori_loop(0, X, body, 0)
+
     def rim(m_ref, e, h):
         build(e, h, 0, -1, X - 1, range(Y + 2))
         spread(m_ref, 0, 0, W, (0,))
         build(e, h, X + 1, 1, 0, range(Y + 2))
         spread(m_ref, X + 1, 0, W, (2,))
 
-        def body(x, carry):
-            build(e, h, x + 1, 0, x, (0, Y + 1))
-            spread(m_ref, x + 1, 0, L, (0, 1, 2))
-            spread(m_ref, x + 1, I1, I1 + L, (0, 1, 2))
-            return carry
-
-        lax.fori_loop(0, X, body, 0)
-
     def clear_pad(ref):
-        for x in range(X + 4):
-            if x < 2 or x >= X + 2:
-                ref[x] = jnp.zeros((2 * C, (Y + 4) * L), BF)
-            else:
-                ref[x, :, 0 : 2 * L] = jnp.zeros((2 * C, 2 * L), BF)
-                ref[x, :, (Y + 2) * L : (Y + 4) * L] = jnp.zeros((2 * C, 2 * L), BF)
+        for x in range(X):
+            ref[x, :, 0 : 2 * L] = jnp.zeros((2 * C, 2 * L), BF)
+            ref[x, :, (Y + 2) * L : (Y + 4) * L] = jnp.zeros((2 * C, 2 * L), BF)
 
     def put_pad(ref, x, v):
         hi, lo = split(v)
-        ref[x + 2, 0:C, 2 * L : (Y + 2) * L] = hi
-        ref[x + 2, C : 2 * C, 2 * L : (Y + 2) * L] = lo
+        ref[x, 0:C, 2 * L : (Y + 2) * L] = hi
+        ref[x, C : 2 * C, 2 * L : (Y + 2) * L] = lo
 
     def correlate(ref):
         acc_ref[...] = jnp.zeros((2 * ROWS, L), F32)
-
-        def body(xp, carry):
+        for xp in range(X + 2):
+            valid = [a for a in range(3) if 0 <= xp - a < X]
             left = jnp.concatenate(
                 [
-                    ref[xp - a + 2, :, (2 - b) * L : (2 - b) * L + W]
-                    for a in range(3)
+                    ref[xp - a, :, (2 - b) * L : (2 - b) * L + W]
+                    for a in valid
                     for b in range(3)
                 ],
                 axis=0,
             )
-            acc_ref[:, 0 : 6 * C] += lax.dot_general(
+            at = valid[0] * 6 * C
+            acc_ref[at : at + left.shape[0], 0 : 6 * C] += lax.dot_general(
                 left, r_ref[xp], (((1,), (1,)), ((), ())), preferred_element_type=F32
             )
-            return carry
-
-        lax.fori_loop(0, X + 2, body, 0)
         pieces = []
         for k in range(9):
             t = acc_ref[2 * k * C : (2 * k + 1) * C] + acc_ref[(2 * k + 1) * C : (2 * k + 2) * C]
@@ -359,7 +367,6 @@
     bring(cin, ec, cbc)
     pass_tiles(0, cbv, hv)
     send_cols(1, cbc)
-    send_faces(1, ec)
     interior(mf_ref, ev, hv)
     clear_pad(agp)
     clear_pad(cvp)
@@ -369,7 +376,10 @@
         return s + jnp.sum(ev[x + 1, :, I0:I1], axis=1, keepdims=True)
 
     in_sum = lax.fori_loop(0, X, vol_sum, jnp.zeros((C, 1), F32))
-    wait_halo(0, ev, hv)
+    wait_edges(0, ev, hv)
+    edges(mf_ref, ev, hv)
+    wait_sides(0, ev, hv)
+    send_faces(1, ec)
     rim(mf_ref, ev, hv)
 
     def gather_conv(x, sums):
@@ -493,6 +503,7 @@
     interior(mb_ref, ea, ha)
     gpart = finish(g_y)
     start(g_f, gpart)
+    edges(mb_ref, ea, ha)
     rim(mb_ref, ea, ha)
 
     def emit(x, carry):
@@ -556,7 +567,7 @@
     e_shape = pltpu.VMEM((X + 2, C, W), F32)
     h_shape = pltpu.VMEM((9, C, L), F32)
     cb_shape = pltpu.VMEM((4, C, L), F32)
-    pad_shape = pltpu.VMEM((X + 4, 2 * C, (Y + 4) * L), BF)
+    pad_shape = pltpu.VMEM((X, 2 * C, (Y + 4) * L), BF)
     m_shape = pltpu.VMEM((ROWS, ROWS), BF)
     line_rows = pltpu.VMEM((ny, 1, L), F32)
     plane_rows = pltpu.VMEM((npl, 1, L), F32)
@@ -587,7 +598,7 @@
             line_rows, plane_rows, line_rows, plane_rows,
             pltpu.VMEM((npl, chunk, L), F32), pltpu.VMEM((ny, chunk, L), F32),
             pltpu.VMEM((npl, chunk, L), F32),
-            dma((5,)), dma((3, 5)), dma((3, 5)), dma((4,)), dma((4,)), dma((3,)), dma((3,)),
+            dma((5,)), dma((3, 6)), dma((3, 6)), dma((4,)), dma((4,)), dma((3,)), dma((3,)),
         ],
         compiler_params=pltpu.CompilerParams(
             collective_id=0, has_side_effects=True, vmem_limit_bytes=24 << 20

time: 55 us -> 48.9 us (0.89)
  Pallas kernels: 54.2 us -> 48.1 us
    pallas_call x1, Pallas kernels: 53.3 us -> 47.2 us  [shards(): pl.pallas_call(functools.partial(kernel, (nx, ny, nz, X, Y), count), out_...]
where the time goes in v4:
time: 48.9 us; the launch traced here: 48.8 us
  Pallas kernels  48.1 us (98%)
  between operations  0.64 us (1%)
    pallas_call x1, Pallas kernels, shards(): pl.pallas_call(functools.partial(kernel, (nx, ny, nz, X, Y), count), out_...  47.2 us

profile of v4, /device:TPU:1, one launch (start us, length us, event | category | flops | bytes accessed | tf_op | source)
XLA Modules:
  0.0 48.8 jit_solution(5579640209309795629)
XLA Ops:
  0.6 47.2 %shard_map.84 = (f32[1024,128]{1,0:T(8,128)S(1)}, f32[432,16]{1,0:T(8,128)S(1)}, f32[1,16]{1,0:T(1,128)S(1)}, f32[1,16]{1,0:T(1,128)S(1)}) custom-call(f32[1024,128]{1,0:T(8,128)} %bitcast.13, f32[1024,128]{1,0:T(8,128)} %bitcast.14, f32[432,16]{1,0:T(8,128)} %bitcast.15, f32[1,16]{1,0:T(1,128)} %bitcast.16, f32[1,16]{1,0:T(1,128)} %bitcast.17), custom_call_target="tpu_custom_call" | custom-call | tf_op jit(solution)/shard_map/pallas_call | solution.py:581
  47.9 0.9 %shard_map.85 = (f32[1024,128]{1,0:T(8,128)}, f32[432,16]{1,0:T(8,128)}, f32[1,16]{1,0:T(1,128)}, f32[1,16]{1,0:T(1,128)}) custom-call(f32[1024,128]{1,0:T(8,128)S(1)} %get-tuple-element.12.refs_0_, f32[432,16]{1,0:T(8,128)S(1)} %get-tuple-element.13.refs_1_, f32[1,16]{1,0:T(1,128)S(1)} %get-tuple-element.14.refs_2_, f32[1,16]{1,0:T(1,128)S(1)} %get-tuple-element.15.refs_3_), custom_call_target="tpu_custom_call" | custom-call | tf_op jit(solution)/shard_map/pallas_call | solution.py:616

commit v5 on v4

--- a/solution.py
+++ b/solution.py
@@ -457,6 +457,10 @@
     for one in plane[2]:
         scatter(one).start()
 
+    part = finish(s_z2)
+    start(s_p2, part)
+    await_bytes(gp_buf.at[pl.ds(0, npl - 1)], grecv.at[0])
+    start(g_y, slots(gp_buf, npl))
     wait_halo(1, ec, hc)
     wait_halo(2, eo, ho)
     for xp in (0, X + 1):
@@ -478,10 +482,6 @@
 
     lax.fori_loop(0, 9, tile_slope, 0)
 
-    part = finish(s_z2)
-    start(s_p2, part)
-    await_bytes(gp_buf.at[pl.ds(0, npl - 1)], grecv.at[0])
-    start(g_y, slots(gp_buf, npl))
     total2 = finish(s_p2)
     gain_grad = unpack(total2, 0)
     shift_grad = unpack(total2, 1)
@@ -500,9 +500,9 @@
         return carry
 
     lax.fori_loop(0, 9, blend_tile, 0)
-    interior(mb_ref, ea, ha)
     gpart = finish(g_y)
     start(g_f, gpart)
+    interior(mb_ref, ea, ha)
     edges(mb_ref, ea, ha)
     rim(mb_ref, ea, ha)
 

time: 48.9 us -> 48.9 us (level)
  no operation moved by 1% of the time
where the time goes in v5:
time: 48.9 us; the launch traced here: 48.8 us
  Pallas kernels  48.1 us (98%)
  between operations  0.64 us (1%)
    pallas_call x1, Pallas kernels, shards(): pl.pallas_call(functools.partial(kernel, (nx, ny, nz, X, Y), count), out_...  47.2 us

profile of v5, /device:TPU:1, one launch (start us, length us, event | category | flops | bytes accessed | tf_op | source)
XLA Modules:
  0.0 48.8 jit_solution(16459024288109300162)
XLA Ops:
  0.6 47.2 %shard_map.84 = (f32[1024,128]{1,0:T(8,128)S(1)}, f32[432,16]{1,0:T(8,128)S(1)}, f32[1,16]{1,0:T(1,128)S(1)}, f32[1,16]{1,0:T(1,128)S(1)}) custom-call(f32[1024,128]{1,0:T(8,128)} %bitcast.13, f32[1024,128]{1,0:T(8,128)} %bitcast.14, f32[432,16]{1,0:T(8,128)} %bitcast.15, f32[1,16]{1,0:T(1,128)} %bitcast.16, f32[1,16]{1,0:T(1,128)} %bitcast.17), custom_call_target="tpu_custom_call" | custom-call | tf_op jit(solution)/shard_map/pallas_call | solution.py:581
  47.9 0.9 %shard_map.85 = (f32[1024,128]{1,0:T(8,128)}, f32[432,16]{1,0:T(8,128)}, f32[1,16]{1,0:T(1,128)}, f32[1,16]{1,0:T(1,128)}) custom-call(f32[1024,128]{1,0:T(8,128)S(1)} %get-tuple-element.12.refs_0_, f32[432,16]{1,0:T(8,128)S(1)} %get-tuple-element.13.refs_1_, f32[1,16]{1,0:T(1,128)S(1)} %get-tuple-element.14.refs_2_, f32[1,16]{1,0:T(1,128)S(1)} %get-tuple-element.15.refs_3_), custom_call_target="tpu_custom_call" | custom-call | tf_op jit(solution)/shard_map/pallas_call | solution.py:616
